TPU v7x, 128 devices: a whole 4x4x4 slice. The times are simulated.
128 devices in a mesh: seq: 8 (over z_hi, x), batch: 16 (over z_lo, y, core).
Axes of the slice: x: 4, y: 4, z: 4 (z_hi: 2, z_lo: 2; z = z_hi * 2 + z_lo), core: 2. Of those that a mesh axis runs over, the one named last changes fastest.
Arguments:
- attn_out: bfloat16 [65536, 2560], P(('seq', 'batch')), may hold values from -200 to 200
- out_grad: bfloat16 [65536, 2560], P(('seq', 'batch')), may hold values from -6 to 6
- master: float32 [2560, 2560], P(('seq', 'batch')), may hold values from -0.125 to 0.125
- moment_one: float32 [2560, 2560], P(('seq', 'batch')), may hold values from -4 to 4
- moment_two: float32 [2560, 2560], P(('seq', 'batch')), may hold values from 0.002 to 0.05
Outputs:
- input_grad: bfloat16 [65536, 2560], P(('seq', 'batch'))
- new_master: float32 [2560, 2560], P(('seq', 'batch'))
- new_moment_one: float32 [2560, 2560], P(('seq', 'batch'))
- new_moment_two: float32 [2560, 2560], P(('seq', 'batch'))
All inputs are finite; a program needn't handle non-finite values.
Results may differ from a plain program's by a relative error of at most 0.01.
Values may be sent and summed in bfloat16 or wider, within the bound.
A program may use at most 128 MiB of HBM per device.

v0:
```python
import jax
import jax.numpy as jnp
from jax import lax
from jax.sharding import Mesh
from jax.sharding import PartitionSpec as P

DIN = 2560
DOUT = 2560
GRAD_BLOCKS = 4
STEP = 10
BATCH = ("batch_0", "batch_1", "batch_2")
SEQ = ("seq_0", "seq_1")
SEQ_BATCH = ("seq_0", "seq_1", "batch_0", "batch_1", "batch_2")


def laid_out(pieces, dim):
    pieces = jnp.moveaxis(pieces, 0, dim)
    lengths = pieces.shape
    return pieces.reshape(*lengths[:dim], lengths[dim] * lengths[dim + 1], *lengths[dim + 2 :])


def copy_for_each(value, axis):
    devices = lax.axis_size(axis)
    return lax.all_to_all(
        jnp.broadcast_to(value[None], (devices, *value.shape)), axis, 0, 0, tiled=True
    )


def gather_directly(value, axis, dim):
    return laid_out(copy_for_each(value, axis), dim)


def by_axis(value, axes):
    for axis in axes:
        value = lax.psum(value, axis)
    return value


def on_device(attn_out, out_grad, master, moment_one, moment_two):
    shard_weight = master.astype(jnp.bfloat16)
    grouped = gather_directly(shard_weight, BATCH, 0)
    projected = lax.dot_general(
        out_grad,
        lax.all_gather(grouped, SEQ, axis=0, tiled=True),
        (((1,), (1,)), ((), ())),
        preferred_element_type=jnp.float32,
    )
    input_grad = projected.astype(jnp.bfloat16)
    block_width = out_grad.shape[1] // GRAD_BLOCKS
    grad_parts = []
    for block in range(GRAD_BLOCKS):
        grad_cols = out_grad[:, block * block_width : (block + 1) * block_width]
        grad_parts.append(
            lax.psum_scatter(
                lax.dot_general(
                    attn_out,
                    grad_cols,
                    (((0,), (0,)), ((), ())),
                    preferred_element_type=jnp.float32,
                ).astype(jnp.bfloat16),
                SEQ_BATCH,
                scatter_dimension=0,
                tiled=True,
            ).astype(jnp.float32)
        )
    weight_grad = jnp.concatenate(grad_parts, axis=1)
    squares = by_axis(jnp.sum(weight_grad * weight_grad), SEQ_BATCH)
    grad_norm = jnp.sqrt(squares) + 1e-06
    limit = jnp.sqrt(jnp.float32(DIN * DOUT))
    clipped = weight_grad * jnp.minimum(jnp.float32(1.0), limit / grad_norm)
    new_one = 0.9 * moment_one + 0.1 * clipped
    new_two = 0.999 * moment_two + 0.001 * clipped * clipped
    first_hat = new_one / (1.0 - 0.9**STEP)
    second_hat = new_two / (1.0 - 0.999**STEP)
    new_master = master - 0.01 * (first_hat / (jnp.sqrt(second_hat) + 1e-08) + 0.1 * master)
    return (input_grad, new_master, new_one, new_two)


def solution(mesh):
    finer = Mesh(
        mesh.devices.reshape(2, 4, 2, 4, 2), ("seq_0", "seq_1", "batch_0", "batch_1", "batch_2")
    )
    in_specs = (
        P(SEQ_BATCH, None),
        P(SEQ_BATCH, None),
        P(SEQ_BATCH, None),
        P(SEQ_BATCH, None),
        P(SEQ_BATCH, None),
    )
    out_specs = (P(SEQ_BATCH, None), P(SEQ_BATCH, None), P(SEQ_BATCH, None), P(SEQ_BATCH, None))
    return jax.shard_map(
        on_device, mesh=finer, in_specs=in_specs, out_specs=out_specs, check_vma=False
    )
```

profile of v0, /device:TPU:1, one launch (start us, length us, event | category | flops | bytes accessed | tf_op | source)
XLA Modules:
  0.0 438.9 jit_solution(13695303821592365688)
XLA Ops:
  7.2 0.0 copy-start
  7.2 0.0 all-reduce.7.cloned.1.call-start
  7.2 1.7 copy-done
  8.9 0.0 copy-start.4
  8.9 5.1 %convolution_convert_fusion = bf16[2560,640]{1,0:T(8,128)(2,1)} fusion(bf16[512,2560]{1,0:T(8,128)(2,1)S(1)} %copy-done, bf16[512,2560]{1,0:T(8,128)(2,1)} %param.6), kind=kOutput, calls=%fused_computation | convolution fusion | flops 1679360000 | bytes 6553600 | tf_op jit(solution)/shard_map/dot_general | solution.py:55
  14.1 0.0 copy-done.4
  14.1 4.0 convolution_convert_fusion.1
  18.0 4.0 convolution_convert_fusion.2
  22.0 4.0 convolution_convert_fusion.3
  26.0 0.0 copy-start.1
  26.0 0.0 copy-start.3
  26.0 0.0 all-reduce.7.cloned.1.call-update
  26.1 0.0 all-gather.2.cloned.1.call-start
  26.1 174.3 %all-reduce.7.cloned.1.call-done = (bf16[2560,640]{1,0:T(8,128)(2,1)}, bf16[2560,640]{1,0:T(8,128)(2,1)}, bf16[2560,640]{1,0:T(8,128)(2,1)}, bf16[2560,640]{1,0:T(8,128)(2,1)}) async-done(((bf16[2560,640]{1,0:T(8,128)(2,1)}, bf16[2560,640]{1,0:T(8,128)(2,1)}, bf16[2560,640]{1,0:T(8,128)(2,1)}, bf16[2560,640]{1,0:T(8,128)(2,1)}), (bf16[2560,640]{1,0:T(8,128)(2,1)}, bf16[2560,640]{1,0:T(8,128)(2,1)}, ...) | async-done | bytes 13107216
  200.4 0.8 constant_dynamic-slice_fusion.2
  201.3 0.8 constant_dynamic-slice_fusion
  202.1 0.7 fusion.6
  202.8 5.9 %psum.35 = f32[]{:T(128)} all-reduce(f32[]{:T(128)} %fusion.6), channel_id=1, replica_groups=mesh['seq_0'=2,'seq_1'=4,'batch_0'=2,'batch_1'=4,'batch_2'=2] {'seq_0'}, use_global_device_ids=true, to_apply=%region_5.0 | all-reduce | flops 1 | bytes 8 | tf_op jit(solution)/shard_map/psum | solution.py:35
  208.7 7.8 %psum.36 = f32[]{:T(128)} all-reduce(f32[]{:T(128)} %psum.35), channel_id=1, replica_groups=mesh['seq_0'=2,'seq_1'=4,'batch_0'=2,'batch_1'=4,'batch_2'=2] {'seq_1'}, use_global_device_ids=true, to_apply=%region_6.0 | all-reduce | flops 1 | bytes 8 | tf_op jit(solution)/shard_map/psum | solution.py:35
  216.5 4.4 psum.37
  220.9 9.0 %psum.38 = f32[]{:T(128)} all-reduce(f32[]{:T(128)} %psum.37), channel_id=1, replica_groups=mesh['seq_0'=2,'seq_1'=4,'batch_0'=2,'batch_1'=4,'batch_2'=2] {'batch_1'}, use_global_device_ids=true, to_apply=%region_8.0 | all-reduce | flops 1 | bytes 8 | tf_op jit(solution)/shard_map/psum | solution.py:35
  229.9 10.0 %psum.39 = f32[]{:T(128)} all-reduce(f32[]{:T(128)} %psum.38), channel_id=1, replica_groups=mesh['seq_0'=2,'seq_1'=4,'batch_0'=2,'batch_1'=4,'batch_2'=2] {'batch_2'}, use_global_device_ids=true, to_apply=%region_9.0 | all-reduce | flops 1 | bytes 8 | tf_op jit(solution)/shard_map/psum | solution.py:35
  240.6 0.0 copy-done.1
  240.6 0.0 copy-done.2
  240.6 0.0 copy-done.3
  240.6 1.0 multiply_subtract_fusion
  241.6 0.1 broadcast_in_dim.2
  241.7 28.6 %all_to_all.5 = bf16[16,20,2560]{2,1,0:T(8,128)(2,1)} all-to-all(bf16[16,20,2560]{2,1,0:T(8,128)(2,1)S(1)} %broadcast_in_dim.2), channel_id=1, replica_groups=mesh['seq_0'=2,'seq_1'=4,'batch_0'=2,'batch_1'=4,'batch_2'=2] {'batch_0'..., dimensions={0} | all-to-all | bytes 3276800 | tf_op jit(solution)/shard_map/all_to_all | solution.py:24
  270.3 3.5 reshape.12
  273.8 0.0 all-gather.2.cloned.1.call-update
  273.9 146.3 %all-gather.2.cloned.1.call-done = bf16[2560,2560]{1,0:T(8,128)(2,1)} async-done(((bf16[320,2560]{1,0:T(8,128)(2,1)}), bf16[2560,2560]{1,0:T(8,128)(2,1)}) %all-gather.2.cloned.1.call-update) | async-done | bytes 13107216 | tf_op jit(solution)/shard_map/all_gather | solution.py:44
  420.2 11.9 %convolution_convert_fusion.4 = bf16[512,2560]{1,0:T(8,128)(2,1)} fusion(bf16[512,2560]{1,0:T(8,128)(2,1)} %param.6, bf16[2560,2560]{1,0:T(8,128)(2,1)} %all-gather.2.cloned.1.call-done), kind=kOutput, calls=%fused_computation.4 | convolution fusion | flops 6712197120 | bytes 18350080 | tf_op jit(solution)/shard_map/dot_general | solution.py:42
  (1 shorter events, 0.0 us)
Async XLA Ops:
  7.2 1.7 copy-start
  7.2 193.3 %all-reduce.7.cloned.1.call-start = ((), (), s32[]{:S(2)}) async-start(), calls=%async_computation.2 | async-start | bytes 26214400
  8.9 5.2 %copy-start.4 = (bf16[512,2560]{1,0:T(8,128)(2,1)S(1)}, bf16[512,2560]{1,0:T(8,128)(2,1)}, u32[]{:S(2)}) copy-start(bf16[512,2560]{1,0:T(8,128)(2,1)} %param.6) | copy-start | bytes 7864324
  26.0 214.5 %copy-start.1 = (f32[20,2560]{1,0:T(8,128)S(1)}, f32[20,2560]{1,0:T(8,128)}, u32[]{:S(2)}) copy-start(f32[20,2560]{1,0:T(8,128)} %param.7) | copy-start | bytes 614404
  26.0 214.6 %copy-start.2 = (f32[20,2560]{1,0:T(8,128)S(1)}, f32[20,2560]{1,0:T(8,128)}, u32[]{:S(2)}) copy-start(f32[20,2560]{1,0:T(8,128)} %param.8) | copy-start | bytes 614404
  26.0 214.6 %copy-start.3 = (f32[20,2560]{1,0:T(8,128)S(1)}, f32[20,2560]{1,0:T(8,128)}, u32[]{:S(2)}) copy-start(f32[20,2560]{1,0:T(8,128)} %param.9) | copy-start | bytes 614404
  26.1 394.1 %all-gather.2.cloned.1.call-start = ((), (), s32[]{:S(2)}) async-start(), calls=%async_computation.1 | async-start | bytes 14745600 | tf_op jit(solution)/shard_map/all_gather | solution.py:44
Sparse Core Ops, SparseCore 0:
  26.2 174.2 all-reduce.6
  274.0 146.1 all-gather.1
where the time goes:
time: 439 us
  waiting for transfers between devices  321 us (73%)
  blocking collectives  65.7 us (15%)
  matrix products  29 us (7%)
  between operations  14.8 us (3%)
  local copies, waits for them, and re-layouts  6.99 us (2%)
    unnamed x3, waiting for transfers between devices  174 us
    all_gather x1, waiting for transfers between devices, on_device(): lax.all_gather(grouped, SEQ, axis=0, tiled=True)  146 us
    psum x5, blocking collectives, by_axis(): value = lax.psum(value, axis)  37.1 us
    all_to_all x1, blocking collectives, copy_for_each(): lax.all_to_all(jnp.broadcast_to(value[None], (devices, *value.shape)), ax...  28.6 us
    dot_general x4, matrix products, on_device(): lax.dot_general(attn_out, grad_cols, (((0,), (0,)), ((), ())), preferred_...  17.1 us
    dot_general x1, matrix products, on_device(): lax.dot_general(out_grad, lax.all_gather(grouped, SEQ, axis=0, tiled=True...  11.9 us
  transfers between devices with their start and end apart: 2, of which 2 were waited for; matrix products, arithmetic and copies ran while one was open for 0% of the time, Pallas kernels for 0%

commit v1 on v0

v1 whole, which is shorter than its diff:
```python
import jax
import jax.numpy as jnp
from jax import lax
from jax.experimental import pallas as pl
from jax.experimental.pallas import tpu as pltpu
from jax.sharding import PartitionSpec as P

DIN = 2560
DOUT = 2560
STEP = 10
TOK = 512
HALF = DIN // 2
ROWS = 80
CHUNKS = 5
OWN = 20
WIDE = 640
BF = jnp.bfloat16
F32 = jnp.float32
MESH = pl.DeviceIdType.MESH
COPIES = 240
AXES = ("y", "x", "z")
SPLITS = ("x", "z", "y")

GATHER = (("x", "y", "z"), ("y", "z", "x"), ("z", "y", "x"), ("x", "z", "y"), ("y", "z", "x"))
SCATTER = (("z", "y", "x"), ("x", "y", "z"), ("y", "z", "x"), ("z", "y", "x"), ("x", "z", "y"))

ORDER = (
    ("p1", 2), ("p1", 1), ("p1", 4), ("p1", 0), ("tr2",), ("rh", 0), ("pre",), ("ags", 3), ("ags", 1),
    ("rh", 2), ("ags", 2), ("rh", 1), ("p1", 3), ("rhm", 0), ("agm", 2), ("rhm", 1), ("rhm", 2), ("agm", 1),
    ("ags", 0), ("agm", 3), ("rm", 0), ("ags", 4), ("agmf", 1), ("rh", 3), ("rh", 4), ("agmf", 2), ("rmm", 0),
    ("rm", 1), ("agm", 0), ("agmf", 3), ("agh", 1), ("rhm", 3), ("rhm", 4), ("rm", 2), ("rmm", 1), ("rs", 0),
    ("agh", 3), ("rm", 4), ("agm", 4), ("agmf", 0), ("rm", 3), ("rmm", 2), ("aghf", 1), ("rmm", 4), ("aghf", 3),
    ("agmf", 4), ("rs", 1), ("agh", 2), ("rmm", 3), ("rs", 4), ("agh", 4), ("rs", 2), ("rs", 3), ("rz", 0),
    ("rz", 1), ("agh", 0), ("dx", 1), ("aghf", 2), ("rz", 2), ("rz", 3), ("rz", 4), ("fin",), ("n", 1),
    ("aghf", 4), ("aghf", 0), ("dx", 3), ("n", 2), ("dx", 2), ("dx", 4), ("n", 3), ("dx", 0), ("end",),
)


def where(chunk, chosen):
    every = pl.ds(0, 2)
    y_col, y_row = chosen.get("y", (every, every))
    z_col, z_row = chosen.get("z", (every, every))
    return (chunk, y_col, z_col, chosen.get("x", pl.ds(0, 4)), z_row, y_row)


DIMS = (("y", 0, 2), ("z", 0, 2), ("x", 0, 4), ("z", 1, 2), ("y", 1, 2))


def landing_shape(gone):
    return (3, *(size for axis, _, size in DIMS if axis not in gone), ROWS, 128)


def halves(axis):
    if axis == "x":
        return pl.ds(0, 2), pl.ds(2, 2)
    return (pl.ds(0, 2), pl.ds(0, 1)), (pl.ds(0, 2), pl.ds(1, 1))


class Body:
    def __init__(self, refs):
        (
            self.attn, self.og, self.master,
            self.dx, self.shard, self.norm,
            self.attn_v, self.attn_t, self.og_v, self.acc, self.grad, self.full, self.r_small, self.dx_acc,
            self.mst, self.give_w, self.stage, self.block, self.summed, self.pieces,
            self.norm_src, self.norm_in,
            self.load_sem, self.send, self.recv, self.pre_recv, self.fin_recv,
            *landings,
        ) = refs
        self.r_large, self.r_mid = landings[:CHUNKS], landings[CHUNKS:]
        self.used = 0
        self.sent = []
        self.late = []
        self.live = {}
        seq = lax.axis_index("seq")
        batch = lax.axis_index("batch")
        self.zh = seq // 4
        self.core = batch % 2
        self.zl = batch // 8
        self.at = {"x": seq % 4, "y": (batch // 2) % 4, "z": self.zh * 2 + self.zl}

    def device(self, x, y, z, core):
        return ((z // 2) * 4 + x, ((z % 2) * 4 + y) * 2 + core)

    def shifted(self, axis, by):
        return (self.at[axis] + by) % 4

    def peer(self, axis, by):
        place = dict(self.at)
        place[axis] = self.shifted(axis, by)
        return self.device(place["x"], place["y"], place["z"], self.core)

    def partner(self):
        return self.device(self.at["x"], self.at["y"], self.at["z"], 1 - self.core)

    def place(self, axis, by=0):
        at = self.shifted(axis, by)
        if axis == "x":
            return at
        if axis == "y":
            return (at % 2, at // 2)
        turned = (at + 2 * self.core) % 4
        col = turned // 2
        return (col, turned + col * (3 - 2 * turned))

    def copy(self, src, dst, device):
        n = self.used
        self.used += 1
        c = pltpu.make_async_remote_copy(
            src_ref=src, dst_ref=dst, send_sem=self.send.at[n], recv_sem=self.recv.at[n],
            device_id=device, device_id_type=MESH,
        )
        c.start()
        self.sent.append(c)
        return c

    def worker_place(self, q):
        z_col = q % 2
        turned = self.zl if z_col == 0 else 3 - self.zl
        return 2 * (self.at["y"] // 2) + q // 2, (turned + 2 * self.zh) % 4, self.zh

    def owner_place(self, i):
        z_row = self.place("z")[1]
        return 2 * (self.at["y"] // 2) + i // 2, 2 * self.core + z_row, i % 2

    def exchange(self, src, dst, recv, place):
        y, z, core = place
        n = self.used
        self.used += 1
        away = pltpu.make_async_remote_copy(
            src_ref=src, dst_ref=dst, send_sem=self.send.at[n], recv_sem=recv,
            device_id=self.device(self.at["x"], y, z, core), device_id_type=MESH,
        )
        here = pltpu.make_async_copy(src, dst, recv)
        mine = (y == self.at["y"]) & (z == self.at["z"]) & (core == self.core)
        pl.when(mine)(here.start)
        pl.when(jnp.logical_not(mine))(away.start)
        self.late.append((jnp.logical_not(mine), away))

    def exchanged(self, like, dst, recv):
        pltpu.make_async_remote_copy(
            src_ref=like, dst_ref=dst, send_sem=self.send.at[0], recv_sem=recv,
            device_id=self.partner(), device_id_type=MESH,
        ).wait_recv()

    def run(self):
        half = pl.multiple_of(self.core * HALF, 128)
        other = pl.multiple_of((1 - self.core) * HALF, 128)
        loads = [
            pltpu.make_async_copy(self.master, self.mst, self.load_sem.at[0]),
            pltpu.make_async_copy(self.attn.at[:, pl.ds(half, HALF)], self.attn_v.at[0], self.load_sem.at[1]),
            pltpu.make_async_copy(self.og, self.og_v.at[pl.ds(0, TOK)], self.load_sem.at[2]),
        ]
        for load in loads:
            load.start()
        barrier = pltpu.get_barrier_semaphore()
        greeted = [self.partner()]
        for axis in AXES:
            greeted += [self.peer(axis, by) for by in (1, 2, 3)]
        for q in range(4):
            for place in (self.worker_place(q), self.owner_place(q)):
                greeted.append(self.device(self.at["x"], *place))
        for device in greeted:
            pl.semaphore_signal(barrier, inc=1, device_id=device, device_id_type=MESH)
        loads[0].wait()
        for q in range(4):
            self.give_w[q] = jnp.concatenate(
                [self.mst[:, 512 * j + 128 * q : 512 * j + 128 * (q + 1)] for j in range(CHUNKS)], axis=1
            ).astype(BF)
        loads[1].wait()
        self.transpose(0)
        pl.semaphore_wait(barrier, len(greeted))

        self.swap_attn = self.copy(
            self.attn.at[:, pl.ds(other, HALF)], self.attn_v.at[1], self.partner()
        )
        slot = (self.at["y"] % 2) * 2 + self.core
        for q in range(4):
            self.exchange(
                self.give_w.at[q], self.stage.at[slot], self.pre_recv.at[slot], self.worker_place(q)
            )
        self.swap_og = [
            self.copy(
                self.og.at[:, pl.ds(512 * j, 512)], self.og_v.at[pl.ds(TOK, TOK), pl.ds(512 * j, 512)],
                self.partner(),
            )
            for j in range(CHUNKS)
        ]
        loads[2].wait()

        sums = [step for step in ORDER if step[0] == "dx"]
        for step in ORDER:
            name = step[0]
            if step == sums[0]:
                name = "dx_first"
            elif step == sums[-1]:
                name = "dx_last"
            elif step in sums:
                name = "dx_more"
            getattr(self, name)(*step[1:])

        for c in self.sent:
            c.wait_send()
        for go, c in self.late:
            pl.when(go)(c.wait_send)

    def transpose(self, which):
        def body(i, carry):
            lanes = pl.ds(pl.multiple_of(i * 128, 128), 128)
            self.attn_t[which, lanes, :] = self.attn_v[which, :, lanes].T
            return carry

        lax.fori_loop(0, HALF // 128, body, 0)

    def tr2(self):
        self.swap_attn.wait_recv()
        self.transpose(1)

    def p1(self, j):
        self.acc[j] = jnp.dot(
            self.attn_t[0], self.og_v[pl.ds(0, TOK), pl.ds(512 * j, 512)], preferred_element_type=F32
        )

    def pre(self):
        for s in range(4):
            self.exchanged(self.give_w.at[0], self.stage.at[s], self.pre_recv.at[s])
            self.block[OWN * s : OWN * (s + 1), :] = self.stage[s].astype(F32)
        here = {axis: self.place(axis) for axis in AXES}
        for j in range(CHUNKS):
            self.full[where(j, here)] = self.block[:, 128 * j : 128 * (j + 1)].astype(BF)

    def ags(self, j):
        axis = GATHER[j][2]
        here = self.full.at[where(j, {a: self.place(a) for a in AXES})]
        self.live["ags", j] = [self.copy(here, here, self.peer(axis, by)) for by in (1, 3, 2)]

    def ring(self, j, axis, fixed, key):
        chosen = {a: self.place(a) for a in fixed}
        split = next(a for a in SPLITS if a != axis and a not in chosen)
        first, second = halves(split)

        def part(by, rows):
            return self.full.at[where(j, {**chosen, axis: self.place(axis, by), split: rows})]

        ahead, behind = self.peer(axis, 1), self.peer(axis, 3)
        top_ahead = self.copy(part(0, first), part(0, first), ahead)
        low_behind = self.copy(part(0, second), part(0, second), behind)
        low_ahead = self.copy(part(0, second), part(0, second), ahead)
        top_behind = self.copy(part(0, first), part(0, first), behind)
        self.live[key] = (top_ahead, low_behind, low_ahead, top_behind, part, first, second)

    def forward(self, axis, key):
        top_ahead, low_behind, low_ahead, top_behind, part, first, second = self.live[key]
        top_ahead.wait_recv()
        on = self.copy(part(3, first), part(3, first), self.peer(axis, 1))
        low_behind.wait_recv()
        back = self.copy(part(1, second), part(1, second), self.peer(axis, 3))
        self.live[key] = (low_ahead, top_behind, on, back)

    def finish(self, key):
        for c in self.live[key]:
            c.wait_recv()

    def agm(self, j):
        self.finish(("ags", j))
        self.ring(j, GATHER[j][1], (GATHER[j][0],), ("agm", j))

    def agmf(self, j):
        self.forward(GATHER[j][1], ("agm", j))

    def agh(self, j):
        self.finish(("agm", j))
        self.ring(j, GATHER[j][0], (), ("agh", j))

    def aghf(self, j):
        self.forward(GATHER[j][0], ("agh", j))

    def dx_dot(self, j, rows):
        left = self.og_v[rows, pl.ds(512 * j, 512)]
        right = jnp.concatenate(
            [self.full[j, q // 2, q % 2].reshape(HALF, 128) for q in range(4)], axis=1
        )
        return lax.dot_general(left, right, (((1,), (1,)), ((), ())), preferred_element_type=F32)

    def dx_first(self, j):
        self.finish(("agh", j))
        self.dx_acc[...] = self.dx_dot(j, pl.ds(0, 2 * TOK))

    def dx_more(self, j):
        self.finish(("agh", j))
        self.dx_acc[...] += self.dx_dot(j, pl.ds(0, 2 * TOK))

    def dx_last(self, j):
        self.finish(("agh", j))
        half = pl.ds(pl.multiple_of(self.core * HALF, 128), HALF)
        theirs, ours = pl.ds(TOK, TOK), pl.ds(0, TOK)
        self.attn_v[1] = (self.dx_acc[theirs, :] + self.dx_dot(j, theirs)).astype(BF)
        give = self.copy(self.attn_v.at[1], self.dx.at[:, half], self.partner())
        self.attn_v[0] = (self.dx_acc[ours, :] + self.dx_dot(j, ours)).astype(BF)
        keep = pltpu.make_async_copy(self.attn_v.at[0], self.dx.at[:, half], self.load_sem.at[3])
        keep.start()
        give.wait_recv()
        keep.wait()

    def rh(self, j):
        self.swap_og[j].wait_recv()
        v = self.acc[j] + jnp.dot(
            self.attn_t[1], self.og_v[pl.ds(TOK, TOK), pl.ds(512 * j, 512)], preferred_element_type=F32
        )
        v = v.astype(BF)
        for q in range(4):
            self.grad[j, q // 2, q % 2] = v[:, 128 * q : 128 * (q + 1)].reshape(4, 2, 2, ROWS, 128)
        self.reduce(j, SCATTER[j][0], (), self.r_large[j], ("rh", j))

    def reduce(self, j, axis, fixed, landing, key):
        chosen = {a: self.place(a) for a in fixed}
        split = next(a for a in SPLITS if a != axis and a not in chosen)
        first, second = halves(split)
        ahead, behind = self.peer(axis, 1), self.peer(axis, 3)

        def part(by, rows):
            return where(j, {**chosen, axis: self.place(axis, by), split: rows})

        def land(slot, rows):
            index = [slot]
            for a, k, size in DIMS:
                if a == split:
                    index.append(rows if a == "x" else rows[k])
                elif a != axis and a not in chosen:
                    index.append(pl.ds(0, size))
            return tuple(index)

        far_ahead = self.copy(self.grad.at[part(2, first)], landing.at[land(0, first)], ahead)
        far_behind = self.copy(self.grad.at[part(2, second)], landing.at[land(0, second)], behind)
        near_ahead = self.copy(self.grad.at[part(1, second)], landing.at[land(1, second)], ahead)
        near_behind = self.copy(self.grad.at[part(3, first)], landing.at[land(2, first)], behind)
        self.live[key] = (far_ahead, far_behind, near_ahead, near_behind, part, land, first, second)

    def pass_on(self, axis, landing, key):
        far_ahead, far_behind, near_ahead, near_behind, part, land, first, second = self.live[key]
        far_ahead.wait_recv()
        at = part(1, first)
        self.grad[at] = (self.grad[at].astype(F32) + landing[land(0, first)].astype(F32)).astype(BF)
        on = self.copy(self.grad.at[at], landing.at[land(1, first)], self.peer(axis, 1))
        far_behind.wait_recv()
        at = part(3, second)
        self.grad[at] = (self.grad[at].astype(F32) + landing[land(0, second)].astype(F32)).astype(BF)
        back = self.copy(self.grad.at[at], landing.at[land(2, second)], self.peer(axis, 3))
        self.live[key] = (near_ahead, near_behind, on, back)

    def rhm(self, j):
        self.pass_on(SCATTER[j][0], self.r_large[j], ("rh", j))

    def rm(self, j):
        self.finish(("rh", j))
        large, mid, small = SCATTER[j]
        at = where(j, {large: self.place(large)})
        landed = self.r_large[j]
        total = self.grad[at].astype(F32) + landed[1].astype(F32)
        self.grad[at] = (total + landed[2].astype(F32)).astype(BF)
        self.reduce(j, mid, (large,), self.r_mid[j], ("rm", j))

    def rmm(self, j):
        self.pass_on(SCATTER[j][1], self.r_mid[j], ("rm", j))

    def rs(self, j):
        self.finish(("rm", j))
        large, mid, small = SCATTER[j]
        chosen = {large: self.place(large), mid: self.place(mid)}
        at = where(j, chosen)
        landed = self.r_mid[j]
        total = self.grad[at].astype(F32) + landed[1].astype(F32)
        self.grad[at] = (total + landed[2].astype(F32)).astype(BF)
        self.live["rs", j] = [
            self.copy(
                self.grad.at[where(j, {**chosen, small: self.place(small, by)})],
                self.r_small.at[j, by - 1],
                self.peer(small, by),
            )
            for by in (1, 3, 2)
        ]

    def rz(self, j):
        self.finish(("rs", j))
        total = self.grad[where(j, {a: self.place(a) for a in AXES})].astype(F32)
        for s in range(3):
            total += self.r_small[j, s].astype(F32)
        self.summed[:, 128 * j : 128 * (j + 1)] = total

    def fin(self):
        total = self.summed[...]
        squares = jnp.sum(total * total, axis=(0, 1), keepdims=True)
        self.norm_src[0] = jnp.broadcast_to(squares, (8, 128))
        self.norm_last = [self.copy(self.norm_src.at[0], self.norm_in.at[0], self.partner())]
        piece = self.place("y")[0] * 2 + self.place("z")[0]
        for i in range(4):
            self.pieces[i] = self.summed[OWN * i : OWN * (i + 1), :]
            self.exchange(
                self.pieces.at[i], self.shard.at[piece], self.fin_recv.at[piece], self.owner_place(i)
            )

    def norm_total(self, k):
        total = self.norm_src[k - 1]
        first = 0 if k == 1 else 3 * k - 5
        for c in self.norm_last:
            c.wait_recv()
        for s in range(len(self.norm_last)):
            total += self.norm_in[first + s]
        return total

    def n(self, k):
        self.norm_src[k] = self.norm_total(k)
        axis = AXES[k - 1]
        self.norm_last = [
            self.copy(self.norm_src.at[k], self.norm_in.at[3 * k - 3 + by], self.peer(axis, by))
            for by in (1, 2, 3)
        ]

    def end(self):
        self.norm_src[4] = self.norm_total(4)
        out = pltpu.make_async_copy(self.norm_src.at[4], self.norm, self.load_sem.at[4])
        out.start()
        for q in range(4):
            self.exchanged(self.pieces.at[0], self.shard.at[q], self.fin_recv.at[q])
        out.wait()


def kernel(*refs):
    Body(refs).run()


def update(*refs):
    dx, *shard_in, dx_out, new_master, new_one, new_two = refs[:10]
    held, *held_in, put_master, put_one, put_two, into_sem, out_sem, small_in, small_out = refs[10:]
    parts = 4
    rows = [pl.ds(TOK // parts * i, TOK // parts) for i in range(parts)]
    into = [pltpu.make_async_copy(dx.at[rows[i]], held.at[i], into_sem.at[i]) for i in range(parts)]
    out = [pltpu.make_async_copy(held.at[i], dx_out.at[rows[i]], out_sem.at[i]) for i in range(parts)]
    loads = [pltpu.make_async_copy(a, b, small_in.at[i]) for i, (a, b) in enumerate(zip(shard_in, held_in))]
    for c in loads[:2] + into[:2] + loads[2:] + into[2:]:
        c.start()
    shard, norm, master, one, two = held_in
    for c in loads[:2] + into[:2]:
        c.wait()
    out[0].start()
    out[1].start()
    limit = jnp.sqrt(jnp.float32(DIN * DOUT))
    clip = jnp.minimum(1.0, limit / (jnp.sqrt(norm[0:1, 0:1]) + 1e-06))
    for c in loads[2:] + into[2:]:
        c.wait()
    out[2].start()
    out[3].start()
    for q in range(4):
        for j in range(CHUNKS):
            cols = slice(512 * j + 128 * q, 512 * j + 128 * (q + 1))
            clipped = shard[q, :, 128 * j : 128 * (j + 1)] * clip
            weight = master[:, cols]
            first = 0.9 * one[:, cols] + 0.1 * clipped
            second = 0.999 * two[:, cols] + 0.001 * clipped * clipped
            first_hat = first / (1.0 - 0.9**STEP)
            second_hat = second / (1.0 - 0.999**STEP)
            put_one[:, cols] = first
            put_two[:, cols] = second
            put_master[:, cols] = weight - 0.01 * (
                first_hat / (jnp.sqrt(second_hat) + 1e-08) + 0.1 * weight
            )
    for i, (a, b) in enumerate(((put_one, new_one), (put_two, new_two), (put_master, new_master))):
        c = pltpu.make_async_copy(a, b, small_out.at[i])
        c.start()
        out.append(c)
    for c in out:
        c.wait()


def on_device(attn_out, out_grad, master, moment_one, moment_two):
    anywhere = pl.BlockSpec(memory_space=pl.ANY)
    vmem = pl.BlockSpec(memory_space=pltpu.VMEM)
    dx, shard, norm = pl.pallas_call(
        kernel,
        out_shape=(
            jax.ShapeDtypeStruct((TOK, DIN), BF),
            jax.ShapeDtypeStruct((4, OWN, WIDE), F32),
            jax.ShapeDtypeStruct((8, 128), F32),
        ),
        in_specs=[anywhere] * 3,
        out_specs=(anywhere,) * 3,
        scratch_shapes=[
            pltpu.VMEM((2, TOK, HALF), BF),
            pltpu.VMEM((2, HALF, TOK), BF),
            pltpu.VMEM((2 * TOK, DOUT), BF),
            pltpu.VMEM((CHUNKS, HALF, 512), F32),
            pltpu.VMEM((CHUNKS, 2, 2, 4, 2, 2, ROWS, 128), BF),
            pltpu.VMEM((CHUNKS, 2, 2, 4, 2, 2, ROWS, 128), BF),
            pltpu.VMEM((CHUNKS, 3, ROWS, 128), BF),
            pltpu.VMEM((2 * TOK, HALF), F32),
            pltpu.VMEM((OWN, DOUT), F32),
            pltpu.VMEM((4, OWN, WIDE), BF),
            pltpu.VMEM((4, OWN, WIDE), BF),
            pltpu.VMEM((ROWS, WIDE), F32),
            pltpu.VMEM((ROWS, WIDE), F32),
            pltpu.VMEM((4, OWN, WIDE), F32),
            pltpu.VMEM((5, 8, 128), F32),
            pltpu.VMEM((10, 8, 128), F32),
            pltpu.SemaphoreType.DMA((5,)),
            pltpu.SemaphoreType.DMA((COPIES,)),
            pltpu.SemaphoreType.DMA((COPIES,)),
            pltpu.SemaphoreType.DMA((4,)),
            pltpu.SemaphoreType.DMA((4,)),
            *(pltpu.VMEM(landing_shape(axes[:1]), BF) for axes in SCATTER),
            *(pltpu.VMEM(landing_shape(axes[:2]), BF) for axes in SCATTER),
        ],
        compiler_params=pltpu.CompilerParams(
            collective_id=0, has_side_effects=True, vmem_limit_bytes=66_000_000
        ),
        cost_estimate=pl.CostEstimate(
            flops=4 * TOK * DIN * DOUT, bytes_accessed=40_000_000, transcendentals=0
        ),
        name="step",
    )(attn_out, out_grad, master)
    part = jax.ShapeDtypeStruct((OWN, DOUT), F32)
    row = pltpu.VMEM((OWN, DOUT), F32)
    return pl.pallas_call(
        update,
        out_shape=(jax.ShapeDtypeStruct((TOK, DIN), BF), part, part, part),
        in_specs=[anywhere] * 6,
        out_specs=(anywhere,) * 4,
        scratch_shapes=[
            pltpu.VMEM((4, TOK // 4, DIN), BF),
            pltpu.VMEM((4, OWN, WIDE), F32),
            pltpu.VMEM((8, 128), F32),
            *(row,) * 6,
            pltpu.SemaphoreType.DMA((4,)),
            pltpu.SemaphoreType.DMA((4,)),
            pltpu.SemaphoreType.DMA((5,)),
            pltpu.SemaphoreType.DMA((3,)),
        ],
        name="update",
    )(dx, shard, norm, master, moment_one, moment_two)


def solution(mesh):
    split = P(("seq", "batch"), None)
    return jax.shard_map(
        on_device, mesh=mesh, in_specs=(split,) * 5, out_specs=(split,) * 4, check_vma=False
    )
```

time: 439 us -> 83.5 us (0.19)
  waiting for transfers between devices: 321 us -> 0 us
  Pallas kernels: 0 us -> 82.6 us
  blocking collectives: 65.7 us -> 0 us
  matrix products: 29 us -> 0 us
  between operations: 14.8 us -> 0.82 us
  local copies, waits for them, and re-layouts: 6.99 us -> 0 us
    unnamed x3 -> x0, waiting for transfers between devices: 174 us -> none
    all_gather x1 -> x0, waiting for transfers between devices: 146 us -> none  [on_device(): lax.all_gather(grouped, SEQ, axis=0, tiled=True)]
    pallas_call x0 -> x2, Pallas kernels: none -> 82.6 us  [the longest x1 79.1 us: on_device(): pl.pallas_call(kernel, out_shape=(jax.ShapeDtypeStruct((TOK, DIN), BF), j...]
    psum x5 -> x0, blocking collectives: 37.1 us -> none  [by_axis(): value = lax.psum(value, axis)]
    dot_general x5 -> x0, matrix products: 29 us -> none  [the longest x4 17.1 us: on_device(): lax.dot_general(attn_out, grad_cols, (((0,), (0,)), ((), ())), preferred_...]
    all_to_all x1 -> x0, blocking collectives: 28.6 us -> none  [copy_for_each(): lax.all_to_all(jnp.broadcast_to(value[None], (devices, *value.shape)), ax...]
  transfers between devices with their start and end apart: 2 -> 0, of which waited for: 2 -> 0; matrix products, arithmetic and copies ran while one was open for 0% -> 0% of each run, Pallas kernels for 0% -> 0%
where the time goes in v1:
time: 83.5 us; the launch traced here: 83.4 us
  Pallas kernels  82.6 us (99%)
    pallas_call x1, Pallas kernels, on_device(): pl.pallas_call(kernel, out_shape=(jax.ShapeDtypeStruct((TOK, DIN), BF), j...  79.1 us
    pallas_call x1, Pallas kernels, on_device(): pl.pallas_call(update, out_shape=(jax.ShapeDtypeStruct((TOK, DIN), BF), p...  3.47 us

profile of v1, /device:TPU:1, one launch (start us, length us, event | category | flops | bytes accessed | tf_op | source)
XLA Modules:
  0.0 83.4 jit_solution(215310631393878490)
XLA Ops:
  0.6 79.1 %step.1 = (bf16[512,2560]{1,0:T(8,128)(2,1)}, f32[4,20,640]{2,1,0:T(8,128)}, f32[8,128]{1,0:T(8,128)}) custom-call(bf16[512,2560]{1,0:T(8,128)(2,1)} %refs_0_.1, bf16[512,2560]{1,0:T(8,128)(2,1)} %refs_1_.1, f32[20,2560]{1,0:T(8,128)} %refs_3_.1), custom_call_target="tpu_custom_call" | custom-call | flops 13421772800 | bytes 40000000 | tf_op jit(solution)/shard_map/step/pallas_call | solution.py:478
  79.8 3.5 %update.1 = (bf16[512,2560]{1,0:T(8,128)(2,1)}, f32[20,2560]{1,0:T(8,128)}, f32[20,2560]{1,0:T(8,128)}, f32[20,2560]{1,0:T(8,128)}) custom-call(bf16[512,2560]{1,0:T(8,128)(2,1)} %get-tuple-element.7.refs_0_, f32[4,20,640]{2,1,0:T(8,128)} %get-tuple-element.8.refs_1_, f32[8,128]{1,0:T(8,128)} %get-tuple-element.9.refs_2_, f32[20,2560]{1,0:T(8,128)} %refs_3_.1, ...), custom_call_target="tpu_custom_call" | custom-call | tf_op jit(solution)/shard_map/update/pallas_call | solution.py:522

commit v2 on v1

--- a/solution.py
+++ b/solution.py
@@ -17,7 +17,8 @@
 BF = jnp.bfloat16
 F32 = jnp.float32
 MESH = pl.DeviceIdType.MESH
-COPIES = 240
+RECEIVES = 84
+SENDS = 19
 AXES = ("y", "x", "z")
 SPLITS = ("x", "z", "y")
 
@@ -64,11 +65,12 @@
             self.attn_v, self.attn_t, self.og_v, self.acc, self.grad, self.full, self.r_small, self.dx_acc,
             self.mst, self.give_w, self.stage, self.block, self.summed, self.pieces,
             self.norm_src, self.norm_in,
-            self.load_sem, self.send, self.recv, self.pre_recv, self.fin_recv,
+            self.load_sem, self.send, self.single, self.recv, self.pre_recv, self.fin_recv,
             *landings,
         ) = refs
         self.r_large, self.r_mid = landings[:CHUNKS], landings[CHUNKS:]
         self.used = 0
+        self.singles = 0
         self.sent = []
         self.late = []
         self.live = {}
@@ -103,16 +105,43 @@
         col = turned // 2
         return (col, turned + col * (3 - 2 * turned))
 
-    def copy(self, src, dst, device):
-        n = self.used
+    def fresh(self):
         self.used += 1
+        return self.used - 1
+
+    def own_send(self):
+        self.singles += 1
+        return self.single.at[self.singles - 1]
+
+    def copy(self, src, dst, device, recv=None, group=None):
+        n = self.fresh() if recv is None else recv
         c = pltpu.make_async_remote_copy(
-            src_ref=src, dst_ref=dst, send_sem=self.send.at[n], recv_sem=self.recv.at[n],
-            device_id=device, device_id_type=MESH,
+            src_ref=src, dst_ref=dst,
+            send_sem=self.own_send() if group is None else self.send.at[group],
+            recv_sem=self.recv.at[n], device_id=device, device_id_type=MESH,
         )
         c.start()
-        self.sent.append(c)
+        if group is None:
+            self.sent.append(c)
         return c
+
+    def take(self, like, n):
+        self.exchanged(like, like, self.recv.at[n])
+
+    def drain(self):
+        for group in range(9):
+            blocks = self.full.at[:, :, :, pl.ds(0, 3)]
+            if group % 3 == 1:
+                blocks = self.full.at[:, pl.ds(0, 1), pl.ds(0, 1), pl.ds(0, 3)]
+            if group % 3 == 2:
+                one = pl.ds(0, 1)
+                blocks = self.full.at[:, one, one, pl.ds(0, 3), one, one]
+            if group > 5:
+                blocks = self.norm_in.at[pl.ds(1, 3)]
+            pltpu.make_async_remote_copy(
+                src_ref=blocks, dst_ref=blocks, send_sem=self.send.at[group], recv_sem=self.recv.at[0],
+                device_id=self.partner(), device_id_type=MESH,
+            ).wait_send()
 
     def worker_place(self, q):
         z_col = q % 2
@@ -125,10 +154,8 @@
 
     def exchange(self, src, dst, recv, place):
         y, z, core = place
-        n = self.used
-        self.used += 1
         away = pltpu.make_async_remote_copy(
-            src_ref=src, dst_ref=dst, send_sem=self.send.at[n], recv_sem=recv,
+            src_ref=src, dst_ref=dst, send_sem=self.own_send(), recv_sem=recv,
             device_id=self.device(self.at["x"], y, z, core), device_id_type=MESH,
         )
         here = pltpu.make_async_copy(src, dst, recv)
@@ -139,7 +166,7 @@
 
     def exchanged(self, like, dst, recv):
         pltpu.make_async_remote_copy(
-            src_ref=like, dst_ref=dst, send_sem=self.send.at[0], recv_sem=recv,
+            src_ref=like, dst_ref=dst, send_sem=self.single.at[0], recv_sem=recv,
             device_id=self.partner(), device_id_type=MESH,
         ).wait_recv()
 
@@ -171,9 +198,15 @@
         self.transpose(0)
         pl.semaphore_wait(barrier, len(greeted))
 
-        self.swap_attn = self.copy(
-            self.attn.at[:, pl.ds(other, HALF)], self.attn_v.at[1], self.partner()
-        )
+        part = HALF // 2
+        self.swap_attn = [
+            self.copy(
+                self.attn.at[:, pl.ds(pl.multiple_of(other + part * i, 128), part)],
+                self.attn_v.at[1, :, pl.ds(part * i, part)],
+                self.partner(),
+            )
+            for i in range(2)
+        ]
         slot = (self.at["y"] % 2) * 2 + self.core
         for q in range(4):
             self.exchange(
@@ -199,22 +232,24 @@
                 name = "dx_more"
             getattr(self, name)(*step[1:])
 
+        self.drain()
         for c in self.sent:
             c.wait_send()
         for go, c in self.late:
             pl.when(go)(c.wait_send)
 
-    def transpose(self, which):
+    def transpose(self, which, first=0, last=10):
         def body(i, carry):
             lanes = pl.ds(pl.multiple_of(i * 128, 128), 128)
             self.attn_t[which, lanes, :] = self.attn_v[which, :, lanes].T
             return carry
 
-        lax.fori_loop(0, HALF // 128, body, 0)
+        lax.fori_loop(first, last, body, 0)
 
     def tr2(self):
-        self.swap_attn.wait_recv()
-        self.transpose(1)
+        for i in range(2):
+            self.swap_attn[i].wait_recv()
+            self.transpose(1, 5 * i, 5 * i + 5)
 
     def p1(self, j):
         self.acc[j] = jnp.dot(
@@ -232,9 +267,12 @@
     def ags(self, j):
         axis = GATHER[j][2]
         here = self.full.at[where(j, {a: self.place(a) for a in AXES})]
-        self.live["ags", j] = [self.copy(here, here, self.peer(axis, by)) for by in (1, 3, 2)]
-
-    def ring(self, j, axis, fixed, key):
+        n = self.fresh()
+        for by in (1, 3, 2):
+            self.copy(here, here, self.peer(axis, by), n, 2)
+        self.live["ags", j] = (n, self.r_small.at[j])
+
+    def ring(self, j, axis, fixed, key, group, both):
         chosen = {a: self.place(a) for a in fixed}
         split = next(a for a in SPLITS if a != axis and a not in chosen)
         first, second = halves(split)
@@ -243,42 +281,43 @@
             return self.full.at[where(j, {**chosen, axis: self.place(axis, by), split: rows})]
 
         ahead, behind = self.peer(axis, 1), self.peer(axis, 3)
-        top_ahead = self.copy(part(0, first), part(0, first), ahead)
-        low_behind = self.copy(part(0, second), part(0, second), behind)
-        low_ahead = self.copy(part(0, second), part(0, second), ahead)
-        top_behind = self.copy(part(0, first), part(0, first), behind)
-        self.live[key] = (top_ahead, low_behind, low_ahead, top_behind, part, first, second)
+        n = self.fresh()
+        top_ahead = self.copy(part(0, first), part(0, first), ahead, None, group)
+        low_behind = self.copy(part(0, second), part(0, second), behind, None, group)
+        self.copy(part(0, second), part(0, second), ahead, n, group)
+        self.copy(part(0, first), part(0, first), behind, n, group)
+        self.live[key] = (top_ahead, low_behind, part, first, second, n, group, both)
 
     def forward(self, axis, key):
-        top_ahead, low_behind, low_ahead, top_behind, part, first, second = self.live[key]
+        top_ahead, low_behind, part, first, second, n, group, both = self.live[key]
         top_ahead.wait_recv()
-        on = self.copy(part(3, first), part(3, first), self.peer(axis, 1))
+        self.copy(part(3, first), part(3, first), self.peer(axis, 1), n, group)
         low_behind.wait_recv()
-        back = self.copy(part(1, second), part(1, second), self.peer(axis, 3))
-        self.live[key] = (low_ahead, top_behind, on, back)
+        self.copy(part(1, second), part(1, second), self.peer(axis, 3), n, group)
+        self.live[key] = (n, both)
 
     def finish(self, key):
-        for c in self.live[key]:
-            c.wait_recv()
+        n, like = self.live[key]
+        self.take(like, n)
 
     def agm(self, j):
         self.finish(("ags", j))
-        self.ring(j, GATHER[j][1], (GATHER[j][0],), ("agm", j))
+        self.ring(j, GATHER[j][1], (GATHER[j][0],), ("agm", j), 1, self.r_mid[j].at[pl.ds(0, 2)])
 
     def agmf(self, j):
         self.forward(GATHER[j][1], ("agm", j))
 
     def agh(self, j):
         self.finish(("agm", j))
-        self.ring(j, GATHER[j][0], (), ("agh", j))
+        self.ring(j, GATHER[j][0], (), ("agh", j), 0, self.r_large[j].at[pl.ds(0, 2)])
 
     def aghf(self, j):
         self.forward(GATHER[j][0], ("agh", j))
 
-    def dx_dot(self, j, rows):
+    def dx_dot(self, j, rows, first=0, last=HALF):
         left = self.og_v[rows, pl.ds(512 * j, 512)]
         right = jnp.concatenate(
-            [self.full[j, q // 2, q % 2].reshape(HALF, 128) for q in range(4)], axis=1
+            [self.full[j, q // 2, q % 2].reshape(HALF, 128)[first:last] for q in range(4)], axis=1
         )
         return lax.dot_general(left, right, (((1,), (1,)), ((), ())), preferred_element_type=F32)
 
@@ -292,15 +331,25 @@
 
     def dx_last(self, j):
         self.finish(("agh", j))
-        half = pl.ds(pl.multiple_of(self.core * HALF, 128), HALF)
-        theirs, ours = pl.ds(TOK, TOK), pl.ds(0, TOK)
-        self.attn_v[1] = (self.dx_acc[theirs, :] + self.dx_dot(j, theirs)).astype(BF)
-        give = self.copy(self.attn_v.at[1], self.dx.at[:, half], self.partner())
-        self.attn_v[0] = (self.dx_acc[ours, :] + self.dx_dot(j, ours)).astype(BF)
-        keep = pltpu.make_async_copy(self.attn_v.at[0], self.dx.at[:, half], self.load_sem.at[3])
-        keep.start()
-        give.wait_recv()
-        keep.wait()
+        start = self.core * HALF
+        gives, keeps = [], []
+        for which, rows in ((1, pl.ds(TOK, TOK)), (0, pl.ds(0, TOK))):
+            for i, (first, last) in enumerate(((0, 512), (512, 1024), (1024, HALF))):
+                cols = pl.ds(first, last - first)
+                done = self.dx_acc[rows, cols] + self.dx_dot(j, rows, first, last)
+                self.attn_v[which, :, cols] = done.astype(BF)
+                src = self.attn_v.at[which, :, cols]
+                to = self.dx.at[:, pl.ds(pl.multiple_of(start + first, 128), last - first)]
+                if which:
+                    gives.append(self.copy(src, to, self.partner()))
+                else:
+                    keep = pltpu.make_async_copy(src, to, self.load_sem.at[5 + i])
+                    keep.start()
+                    keeps.append(keep)
+        for c in gives:
+            c.wait_recv()
+        for c in keeps:
+            c.wait()
 
     def rh(self, j):
         self.swap_og[j].wait_recv()
@@ -310,9 +359,9 @@
         v = v.astype(BF)
         for q in range(4):
             self.grad[j, q // 2, q % 2] = v[:, 128 * q : 128 * (q + 1)].reshape(4, 2, 2, ROWS, 128)
-        self.reduce(j, SCATTER[j][0], (), self.r_large[j], ("rh", j))
-
-    def reduce(self, j, axis, fixed, landing, key):
+        self.reduce(j, SCATTER[j][0], (), self.r_large[j], ("rh", j), 3)
+
+    def reduce(self, j, axis, fixed, landing, key, group):
         chosen = {a: self.place(a) for a in fixed}
         split = next(a for a in SPLITS if a != axis and a not in chosen)
         first, second = halves(split)
@@ -330,23 +379,30 @@
                     index.append(pl.ds(0, size))
             return tuple(index)
 
-        far_ahead = self.copy(self.grad.at[part(2, first)], landing.at[land(0, first)], ahead)
-        far_behind = self.copy(self.grad.at[part(2, second)], landing.at[land(0, second)], behind)
-        near_ahead = self.copy(self.grad.at[part(1, second)], landing.at[land(1, second)], ahead)
-        near_behind = self.copy(self.grad.at[part(3, first)], landing.at[land(2, first)], behind)
-        self.live[key] = (far_ahead, far_behind, near_ahead, near_behind, part, land, first, second)
+        n = self.fresh()
+
+        def send(by, rows, slot, device, recv):
+            return self.copy(
+                self.grad.at[part(by, rows)], landing.at[land(slot, rows)], device, recv, group
+            )
+
+        far_ahead = send(2, first, 0, ahead, None)
+        far_behind = send(2, second, 0, behind, None)
+        send(1, second, 1, ahead, n)
+        send(3, first, 2, behind, n)
+        self.live[key] = (far_ahead, far_behind, part, land, first, second, n, send)
 
     def pass_on(self, axis, landing, key):
-        far_ahead, far_behind, near_ahead, near_behind, part, land, first, second = self.live[key]
+        far_ahead, far_behind, part, land, first, second, n, send = self.live[key]
         far_ahead.wait_recv()
         at = part(1, first)
         self.grad[at] = (self.grad[at].astype(F32) + landing[land(0, first)].astype(F32)).astype(BF)
-        on = self.copy(self.grad.at[at], landing.at[land(1, first)], self.peer(axis, 1))
+        send(1, first, 1, self.peer(axis, 1), n)
         far_behind.wait_recv()
         at = part(3, second)
         self.grad[at] = (self.grad[at].astype(F32) + landing[land(0, second)].astype(F32)).astype(BF)
-        back = self.copy(self.grad.at[at], landing.at[land(2, second)], self.peer(axis, 3))
-        self.live[key] = (near_ahead, near_behind, on, back)
+        send(3, second, 2, self.peer(axis, 3), n)
+        self.live[key] = (n, landing.at[pl.ds(0, 2)])
 
     def rhm(self, j):
         self.pass_on(SCATTER[j][0], self.r_large[j], ("rh", j))
@@ -358,7 +414,7 @@
         landed = self.r_large[j]
         total = self.grad[at].astype(F32) + landed[1].astype(F32)
         self.grad[at] = (total + landed[2].astype(F32)).astype(BF)
-        self.reduce(j, mid, (large,), self.r_mid[j], ("rm", j))
+        self.reduce(j, mid, (large,), self.r_mid[j], ("rm", j), 4)
 
     def rmm(self, j):
         self.pass_on(SCATTER[j][1], self.r_mid[j], ("rm", j))
@@ -371,14 +427,11 @@
         landed = self.r_mid[j]
         total = self.grad[at].astype(F32) + landed[1].astype(F32)
         self.grad[at] = (total + landed[2].astype(F32)).astype(BF)
-        self.live["rs", j] = [
-            self.copy(
-                self.grad.at[where(j, {**chosen, small: self.place(small, by)})],
-                self.r_small.at[j, by - 1],
-                self.peer(small, by),
-            )
-            for by in (1, 3, 2)
-        ]
+        n = self.fresh()
+        for by in (1, 3, 2):
+            at = where(j, {**chosen, small: self.place(small, by)})
+            self.copy(self.grad.at[at], self.r_small.at[j, by - 1], self.peer(small, by), n, 5)
+        self.live["rs", j] = (n, self.r_small.at[j])
 
     def rz(self, j):
         self.finish(("rs", j))
@@ -391,7 +444,8 @@
         total = self.summed[...]
         squares = jnp.sum(total * total, axis=(0, 1), keepdims=True)
         self.norm_src[0] = jnp.broadcast_to(squares, (8, 128))
-        self.norm_last = [self.copy(self.norm_src.at[0], self.norm_in.at[0], self.partner())]
+        self.norm_last = self.fresh()
+        self.copy(self.norm_src.at[0], self.norm_in.at[0], self.partner(), self.norm_last)
         piece = self.place("y")[0] * 2 + self.place("z")[0]
         for i in range(4):
             self.pieces[i] = self.summed[OWN * i : OWN * (i + 1), :]
@@ -401,20 +455,19 @@
 
     def norm_total(self, k):
         total = self.norm_src[k - 1]
-        first = 0 if k == 1 else 3 * k - 5
-        for c in self.norm_last:
-            c.wait_recv()
-        for s in range(len(self.norm_last)):
+        first, count = (0, 1) if k == 1 else (3 * k - 5, 3)
+        self.take(self.norm_in.at[pl.ds(first, count)], self.norm_last)
+        for s in range(count):
             total += self.norm_in[first + s]
         return total
 
     def n(self, k):
         self.norm_src[k] = self.norm_total(k)
         axis = AXES[k - 1]
-        self.norm_last = [
-            self.copy(self.norm_src.at[k], self.norm_in.at[3 * k - 3 + by], self.peer(axis, by))
-            for by in (1, 2, 3)
-        ]
+        self.norm_last = self.fresh()
+        for by in (1, 2, 3):
+            to = self.norm_in.at[3 * k - 3 + by]
+            self.copy(self.norm_src.at[k], to, self.peer(axis, by), self.norm_last, 5 + k)
 
     def end(self):
         self.norm_src[4] = self.norm_total(4)
@@ -426,7 +479,9 @@
 
 
 def kernel(*refs):
-    Body(refs).run()
+    body = Body(refs)
+    body.run()
+    assert body.used == RECEIVES and body.singles == SENDS, (body.used, body.singles)
 
 
 def update(*refs):
@@ -501,9 +556,10 @@
             pltpu.VMEM((4, OWN, WIDE), F32),
             pltpu.VMEM((5, 8, 128), F32),
             pltpu.VMEM((10, 8, 128), F32),
-            pltpu.SemaphoreType.DMA((5,)),
-            pltpu.SemaphoreType.DMA((COPIES,)),
-            pltpu.SemaphoreType.DMA((COPIES,)),
+            pltpu.SemaphoreType.DMA((8,)),
+            pltpu.SemaphoreType.DMA((9,)),
+            pltpu.SemaphoreType.DMA((SENDS,)),
+            pltpu.SemaphoreType.DMA((RECEIVES,)),
             pltpu.SemaphoreType.DMA((4,)),
             pltpu.SemaphoreType.DMA((4,)),
             *(pltpu.VMEM(landing_shape(axes[:1]), BF) for axes in SCATTER),

time: 83.5 us -> 79.3 us (0.950)
  Pallas kernels: 82.6 us -> 78.3 us
    pallas_call x1, Pallas kernels: 79.1 us -> 74.9 us  [on_device(): pl.pallas_call(kernel, out_shape=(jax.ShapeDtypeStruct((TOK, DIN), BF), j...]
where the time goes in v2:
time: 79.3 us; the launch traced here: 79.1 us
  Pallas kernels  78.3 us (99%)
  between operations  0.8 us (1%)
    pallas_call x1, Pallas kernels, on_device(): pl.pallas_call(kernel, out_shape=(jax.ShapeDtypeStruct((TOK, DIN), BF), j...  74.9 us
    pallas_call x1, Pallas kernels, on_device(): pl.pallas_call(update, out_shape=(jax.ShapeDtypeStruct((TOK, DIN), BF), p...  3.47 us

profile of v2, /device:TPU:1, one launch (start us, length us, event | category | flops | bytes accessed | tf_op | source)
XLA Modules:
  0.0 79.1 jit_solution(1332641504325979733)
XLA Ops:
  0.6 74.9 %step.1 = (bf16[512,2560]{1,0:T(8,128)(2,1)}, f32[4,20,640]{2,1,0:T(8,128)}, f32[8,128]{1,0:T(8,128)}) custom-call(bf16[512,2560]{1,0:T(8,128)(2,1)} %refs_0_.1, bf16[512,2560]{1,0:T(8,128)(2,1)} %refs_1_.1, f32[20,2560]{1,0:T(8,128)} %refs_3_.1), custom_call_target="tpu_custom_call" | custom-call | flops 13421772800 | bytes 40000000 | tf_op jit(solution)/shard_map/step/pallas_call | solution.py:533
  75.5 3.5 %update.1 = (bf16[512,2560]{1,0:T(8,128)(2,1)}, f32[20,2560]{1,0:T(8,128)}, f32[20,2560]{1,0:T(8,128)}, f32[20,2560]{1,0:T(8,128)}) custom-call(bf16[512,2560]{1,0:T(8,128)(2,1)} %get-tuple-element.7.refs_0_, f32[4,20,640]{2,1,0:T(8,128)} %get-tuple-element.8.refs_1_, f32[8,128]{1,0:T(8,128)} %get-tuple-element.9.refs_2_, f32[20,2560]{1,0:T(8,128)} %refs_3_.1, ...), custom_call_target="tpu_custom_call" | custom-call | tf_op jit(solution)/shard_map/update/pallas_call | solution.py:578

commit v3 on v2

--- a/solution.py
+++ b/solution.py
@@ -487,24 +487,26 @@
 def update(*refs):
     dx, *shard_in, dx_out, new_master, new_one, new_two = refs[:10]
     held, *held_in, put_master, put_one, put_two, into_sem, out_sem, small_in, small_out = refs[10:]
-    parts = 4
+    parts = 8
     rows = [pl.ds(TOK // parts * i, TOK // parts) for i in range(parts)]
     into = [pltpu.make_async_copy(dx.at[rows[i]], held.at[i], into_sem.at[i]) for i in range(parts)]
     out = [pltpu.make_async_copy(held.at[i], dx_out.at[rows[i]], out_sem.at[i]) for i in range(parts)]
     loads = [pltpu.make_async_copy(a, b, small_in.at[i]) for i, (a, b) in enumerate(zip(shard_in, held_in))]
-    for c in loads[:2] + into[:2] + loads[2:] + into[2:]:
+    for c in loads[:2] + into[:4] + loads[2:] + into[4:]:
         c.start()
     shard, norm, master, one, two = held_in
-    for c in loads[:2] + into[:2]:
+    for c in loads[:2]:
         c.wait()
-    out[0].start()
-    out[1].start()
+    for i in range(4):
+        into[i].wait()
+        out[i].start()
     limit = jnp.sqrt(jnp.float32(DIN * DOUT))
     clip = jnp.minimum(1.0, limit / (jnp.sqrt(norm[0:1, 0:1]) + 1e-06))
-    for c in loads[2:] + into[2:]:
+    for i in range(4, parts):
+        into[i].wait()
+        out[i].start()
+    for c in loads[2:]:
         c.wait()
-    out[2].start()
-    out[3].start()
     for q in range(4):
         for j in range(CHUNKS):
             cols = slice(512 * j + 128 * q, 512 * j + 128 * (q + 1))
@@ -581,12 +583,12 @@
         in_specs=[anywhere] * 6,
         out_specs=(anywhere,) * 4,
         scratch_shapes=[
-            pltpu.VMEM((4, TOK // 4, DIN), BF),
+            pltpu.VMEM((8, TOK // 8, DIN), BF),
             pltpu.VMEM((4, OWN, WIDE), F32),
             pltpu.VMEM((8, 128), F32),
             *(row,) * 6,
-            pltpu.SemaphoreType.DMA((4,)),
-            pltpu.SemaphoreType.DMA((4,)),
+            pltpu.SemaphoreType.DMA((8,)),
+            pltpu.SemaphoreType.DMA((8,)),
             pltpu.SemaphoreType.DMA((5,)),
             pltpu.SemaphoreType.DMA((3,)),
         ],

time: 79.3 us -> 79 us (level)
  no operation moved by 1% of the time
where the time goes in v3:
time: 79 us; the launch traced here: 78.9 us
  Pallas kernels  78.1 us (99%)
  between operations  0.8 us (1%)
    pallas_call x1, Pallas kernels, on_device(): pl.pallas_call(kernel, out_shape=(jax.ShapeDtypeStruct((TOK, DIN), BF), j...  74.9 us
    pallas_call x1, Pallas kernels, on_device(): pl.pallas_call(update, out_shape=(jax.ShapeDtypeStruct((TOK, DIN), BF), p...  3.25 us

profile of v3, /device:TPU:1, one launch (start us, length us, event | category | flops | bytes accessed | tf_op | source)
XLA Modules:
  0.0 78.9 jit_solution(2730085160878076770)
XLA Ops:
  0.6 74.9 %step.1 = (bf16[512,2560]{1,0:T(8,128)(2,1)}, f32[4,20,640]{2,1,0:T(8,128)}, f32[8,128]{1,0:T(8,128)}) custom-call(bf16[512,2560]{1,0:T(8,128)(2,1)} %refs_0_.1, bf16[512,2560]{1,0:T(8,128)(2,1)} %refs_1_.1, f32[20,2560]{1,0:T(8,128)} %refs_3_.1), custom_call_target="tpu_custom_call" | custom-call | flops 13421772800 | bytes 40000000 | tf_op jit(solution)/shard_map/step/pallas_call | solution.py:535
  75.5 3.2 %update.1 = (bf16[512,2560]{1,0:T(8,128)(2,1)}, f32[20,2560]{1,0:T(8,128)}, f32[20,2560]{1,0:T(8,128)}, f32[20,2560]{1,0:T(8,128)}) custom-call(bf16[512,2560]{1,0:T(8,128)(2,1)} %get-tuple-element.7.refs_0_, f32[4,20,640]{2,1,0:T(8,128)} %get-tuple-element.8.refs_1_, f32[8,128]{1,0:T(8,128)} %get-tuple-element.9.refs_2_, f32[20,2560]{1,0:T(8,128)} %refs_3_.1, ...), custom_call_target="tpu_custom_call" | custom-call | tf_op jit(solution)/shard_map/update/pallas_call | solution.py:580

commit v4 on v3

--- a/solution.py
+++ b/solution.py
@@ -17,8 +17,8 @@
 BF = jnp.bfloat16
 F32 = jnp.float32
 MESH = pl.DeviceIdType.MESH
-RECEIVES = 84
-SENDS = 19
+RECEIVES = 83
+SENDS = 25
 AXES = ("y", "x", "z")
 SPLITS = ("x", "z", "y")
 
@@ -32,8 +32,8 @@
     ("rm", 1), ("agm", 0), ("agmf", 3), ("agh", 1), ("rhm", 3), ("rhm", 4), ("rm", 2), ("rmm", 1), ("rs", 0),
     ("agh", 3), ("rm", 4), ("agm", 4), ("agmf", 0), ("rm", 3), ("rmm", 2), ("aghf", 1), ("rmm", 4), ("aghf", 3),
     ("agmf", 4), ("rs", 1), ("agh", 2), ("rmm", 3), ("rs", 4), ("agh", 4), ("rs", 2), ("rs", 3), ("rz", 0),
-    ("rz", 1), ("agh", 0), ("dx", 1), ("aghf", 2), ("rz", 2), ("rz", 3), ("rz", 4), ("fin",), ("n", 1),
-    ("aghf", 4), ("aghf", 0), ("dx", 3), ("n", 2), ("dx", 2), ("dx", 4), ("n", 3), ("dx", 0), ("end",),
+    ("rz", 1), ("agh", 0), ("dx", 1), ("aghf", 2), ("rz", 2), ("rz", 3), ("rz", 4), ("fin",), ("aghf", 4),
+    ("aghf", 0), ("dx", 3), ("n", 1), ("dx", 2), ("dx", 4), ("n", 2), ("dx", 0), ("end",),
 )
 
 
@@ -92,6 +92,9 @@
         place[axis] = self.shifted(axis, by)
         return self.device(place["x"], place["y"], place["z"], self.core)
 
+    def across(self, by):
+        return self.device(self.at["x"], self.shifted("y", by), self.at["z"], 1 - self.core)
+
     def partner(self):
         return self.device(self.at["x"], self.at["y"], self.at["z"], 1 - self.core)
 
@@ -129,7 +132,7 @@
         self.exchanged(like, like, self.recv.at[n])
 
     def drain(self):
-        for group in range(9):
+        for group in range(8):
             blocks = self.full.at[:, :, :, pl.ds(0, 3)]
             if group % 3 == 1:
                 blocks = self.full.at[:, pl.ds(0, 1), pl.ds(0, 1), pl.ds(0, 3)]
@@ -181,7 +184,7 @@
         for load in loads:
             load.start()
         barrier = pltpu.get_barrier_semaphore()
-        greeted = [self.partner()]
+        greeted = [self.partner()] + [self.across(by) for by in (1, 2, 3)]
         for axis in AXES:
             greeted += [self.peer(axis, by) for by in (1, 2, 3)]
         for q in range(4):
@@ -445,7 +448,10 @@
         squares = jnp.sum(total * total, axis=(0, 1), keepdims=True)
         self.norm_src[0] = jnp.broadcast_to(squares, (8, 128))
         self.norm_last = self.fresh()
-        self.copy(self.norm_src.at[0], self.norm_in.at[0], self.partner(), self.norm_last)
+        to = [self.partner()]
+        to += [self.peer("y", by) for by in (1, 2, 3)] + [self.across(by) for by in (1, 2, 3)]
+        for slot, device in enumerate(to):
+            self.copy(self.norm_src.at[0], self.norm_in.at[slot], device, self.norm_last)
         piece = self.place("y")[0] * 2 + self.place("z")[0]
         for i in range(4):
             self.pieces[i] = self.summed[OWN * i : OWN * (i + 1), :]
@@ -455,7 +461,7 @@
 
     def norm_total(self, k):
         total = self.norm_src[k - 1]
-        first, count = (0, 1) if k == 1 else (3 * k - 5, 3)
+        first, count = (0, 7) if k == 1 else (3 * k + 1, 3)
         self.take(self.norm_in.at[pl.ds(first, count)], self.norm_last)
         for s in range(count):
             total += self.norm_in[first + s]
@@ -463,15 +469,15 @@
 
     def n(self, k):
         self.norm_src[k] = self.norm_total(k)
-        axis = AXES[k - 1]
+        axis = AXES[k]
         self.norm_last = self.fresh()
         for by in (1, 2, 3):
-            to = self.norm_in.at[3 * k - 3 + by]
+            to = self.norm_in.at[3 * k + 3 + by]
             self.copy(self.norm_src.at[k], to, self.peer(axis, by), self.norm_last, 5 + k)
 
     def end(self):
-        self.norm_src[4] = self.norm_total(4)
-        out = pltpu.make_async_copy(self.norm_src.at[4], self.norm, self.load_sem.at[4])
+        self.norm_src[3] = self.norm_total(3)
+        out = pltpu.make_async_copy(self.norm_src.at[3], self.norm, self.load_sem.at[4])
         out.start()
         for q in range(4):
             self.exchanged(self.pieces.at[0], self.shard.at[q], self.fin_recv.at[q])
@@ -556,10 +562,10 @@
             pltpu.VMEM((ROWS, WIDE), F32),
             pltpu.VMEM((ROWS, WIDE), F32),
             pltpu.VMEM((4, OWN, WIDE), F32),
-            pltpu.VMEM((5, 8, 128), F32),
-            pltpu.VMEM((10, 8, 128), F32),
+            pltpu.VMEM((4, 8, 128), F32),
+            pltpu.VMEM((13, 8, 128), F32),
             pltpu.SemaphoreType.DMA((8,)),
-            pltpu.SemaphoreType.DMA((9,)),
+            pltpu.SemaphoreType.DMA((8,)),
             pltpu.SemaphoreType.DMA((SENDS,)),
             pltpu.SemaphoreType.DMA((RECEIVES,)),
             pltpu.SemaphoreType.DMA((4,)),

time: 79 us -> 76.9 us (0.973)
  Pallas kernels: 78.1 us -> 76 us
    pallas_call x1, Pallas kernels: 74.9 us -> 72.8 us  [on_device(): pl.pallas_call(kernel, out_shape=(jax.ShapeDtypeStruct((TOK, DIN), BF), j...]
where the time goes in v4:
time: 76.9 us; the launch traced here: 76.8 us
  Pallas kernels  76 us (99%)
  between operations  0.8 us (1%)
    pallas_call x1, Pallas kernels, on_device(): pl.pallas_call(kernel, out_shape=(jax.ShapeDtypeStruct((TOK, DIN), BF), j...  72.8 us
    pallas_call x1, Pallas kernels, on_device(): pl.pallas_call(update, out_shape=(jax.ShapeDtypeStruct((TOK, DIN), BF), p...  3.25 us

profile of v4, /device:TPU:1, one launch (start us, length us, event | category | flops | bytes accessed | tf_op | source)
XLA Modules:
  0.0 76.8 jit_solution(12561347541208571012)
XLA Ops:
  0.6 72.8 %step.1 = (bf16[512,2560]{1,0:T(8,128)(2,1)}, f32[4,20,640]{2,1,0:T(8,128)}, f32[8,128]{1,0:T(8,128)}) custom-call(bf16[512,2560]{1,0:T(8,128)(2,1)} %refs_0_.1, bf16[512,2560]{1,0:T(8,128)(2,1)} %refs_1_.1, f32[20,2560]{1,0:T(8,128)} %refs_3_.1), custom_call_target="tpu_custom_call" | custom-call | flops 13421772800 | bytes 40000000 | tf_op jit(solution)/shard_map/step/pallas_call | solution.py:541
  73.4 3.2 %update.1 = (bf16[512,2560]{1,0:T(8,128)(2,1)}, f32[20,2560]{1,0:T(8,128)}, f32[20,2560]{1,0:T(8,128)}, f32[20,2560]{1,0:T(8,128)}) custom-call(bf16[512,2560]{1,0:T(8,128)(2,1)} %get-tuple-element.7.refs_0_, f32[4,20,640]{2,1,0:T(8,128)} %get-tuple-element.8.refs_1_, f32[8,128]{1,0:T(8,128)} %get-tuple-element.9.refs_2_, f32[20,2560]{1,0:T(8,128)} %refs_3_.1, ...), custom_call_target="tpu_custom_call" | custom-call | tf_op jit(solution)/shard_map/update/pallas_call | solution.py:586

commit v5 on v4

--- a/solution.py
+++ b/solution.py
@@ -181,8 +181,6 @@
             pltpu.make_async_copy(self.attn.at[:, pl.ds(half, HALF)], self.attn_v.at[0], self.load_sem.at[1]),
             pltpu.make_async_copy(self.og, self.og_v.at[pl.ds(0, TOK)], self.load_sem.at[2]),
         ]
-        for load in loads:
-            load.start()
         barrier = pltpu.get_barrier_semaphore()
         greeted = [self.partner()] + [self.across(by) for by in (1, 2, 3)]
         for axis in AXES:
@@ -190,8 +188,10 @@
         for q in range(4):
             for place in (self.worker_place(q), self.owner_place(q)):
                 greeted.append(self.device(self.at["x"], *place))
-        for device in greeted:
+        for device in reversed(greeted):
             pl.semaphore_signal(barrier, inc=1, device_id=device, device_id_type=MESH)
+        for load in loads:
+            load.start()
         loads[0].wait()
         for q in range(4):
             self.give_w[q] = jnp.concatenate(

time: 76.9 us -> 77.7 us (1.010)
  Pallas kernels: 76 us -> 76.8 us
where the time goes in v5:
time: 77.7 us; the launch traced here: 77.6 us
  Pallas kernels  76.8 us (99%)
  between operations  0.8 us (1%)
    pallas_call x1, Pallas kernels, on_device(): pl.pallas_call(kernel, out_shape=(jax.ShapeDtypeStruct((TOK, DIN), BF), j...  73.5 us
    pallas_call x1, Pallas kernels, on_device(): pl.pallas_call(update, out_shape=(jax.ShapeDtypeStruct((TOK, DIN), BF), p...  3.25 us

profile of v5, /device:TPU:1, one launch (start us, length us, event | category | flops | bytes accessed | tf_op | source)
XLA Modules:
  0.0 77.6 jit_solution(2028534282432908382)
XLA Ops:
  0.6 73.5 %step.1 = (bf16[512,2560]{1,0:T(8,128)(2,1)}, f32[4,20,640]{2,1,0:T(8,128)}, f32[8,128]{1,0:T(8,128)}) custom-call(bf16[512,2560]{1,0:T(8,128)(2,1)} %refs_0_.1, bf16[512,2560]{1,0:T(8,128)(2,1)} %refs_1_.1, f32[20,2560]{1,0:T(8,128)} %refs_3_.1), custom_call_target="tpu_custom_call" | custom-call | flops 13421772800 | bytes 40000000 | tf_op jit(solution)/shard_map/step/pallas_call | solution.py:541
  74.2 3.2 %update.1 = (bf16[512,2560]{1,0:T(8,128)(2,1)}, f32[20,2560]{1,0:T(8,128)}, f32[20,2560]{1,0:T(8,128)}, f32[20,2560]{1,0:T(8,128)}) custom-call(bf16[512,2560]{1,0:T(8,128)(2,1)} %get-tuple-element.7.refs_0_, f32[4,20,640]{2,1,0:T(8,128)} %get-tuple-element.8.refs_1_, f32[8,128]{1,0:T(8,128)} %get-tuple-element.9.refs_2_, f32[20,2560]{1,0:T(8,128)} %refs_3_.1, ...), custom_call_target="tpu_custom_call" | custom-call | tf_op jit(solution)/shard_map/update/pallas_call | solution.py:586
